TPU v7x, 32 devices: a whole 2x2x4 slice. The times are simulated.
32 devices in a mesh: grp: 2 (over x), tm: 16 (over z, y, core).
Axes of the slice: x: 2, y: 2, z: 4, core: 2. Of those that a mesh axis runs over, the one named last changes fastest.
Arguments:
- visibilities: float32 [2048, 2, 16, 1024], P('tm', None, 'grp'), parts along dimension 2, may hold values from -6 to 6
- redundancy: int32 [2048], P('grp'), parts along dimension 0, may hold values from 0 to 511, as said below
- mode_counts: int32 [2048], P('tm'), may hold values from 4 to 16
- filters: bfloat16 [2048, 2, 16, 16, 512], P('tm', None, None, 'grp'), parts along dimension 3, may hold values from -0.0625 to 0.0625
Outputs:
- mmodes: float32 [2048, 2, 16, 512], P('tm', None, 'grp'), parts along dimension 2
- modes: float32 [2048, 2, 32], P('tm', None, 'grp'), parts along dimension 2
There are 2 independent parts, one for each index of `grp`. A program takes and returns all parts, laid end to end along the dimension named above; an argument that names none is the same for every part. Nothing has to cross between parts.
Inputs may be any that keep to these rules, and one draw needn't show every extreme that they name: `redundancy`: each of the 512 unique baselines is named by at least one raw baseline.
All inputs are finite; a program needn't handle non-finite values.
Results may differ from a plain program's by a relative error of at most 0.0029.
Values sent between devices are 32-bit elements; how exact they have to be, the bound alone decides.
A program may use at most 128 MiB of HBM per device.

v0:
```python
import functools

import numpy as np
import jax
import jax.numpy as jnp
from jax import lax
from jax.experimental import pallas as pl
from jax.experimental.pallas import tpu as pltpu
from jax.sharding import PartitionSpec as P

MESH = pl.DeviceIdType.MESH
LANES = 128
BLOCKS = 4
NT = (((1,), (1,)), ((), ()))


def split_bf16(x):
    high = x.astype(jnp.bfloat16)
    return high, (x - high.astype(jnp.float32)).astype(jnp.bfloat16)


def cmul_const(z, c):
    re, im = z
    if c == 1:
        return z
    if c == -1j:
        return im, -re
    cr, ci = float(c.real), float(c.imag)
    if abs(abs(cr) - abs(ci)) < 1e-12:
        return (re - im) * cr if ci * cr > 0 else (re + im) * cr, (re + im) * cr if ci * cr > 0 else (im - re) * cr
    return re * cr - im * ci, re * ci + im * cr


def small_fft(zs):
    n = len(zs)
    if n == 1:
        return zs
    half = n // 2
    tops = [(a[0] + b[0], a[1] + b[1]) for a, b in zip(zs[:half], zs[half:])]
    lows = [(a[0] - b[0], a[1] - b[1]) for a, b in zip(zs[:half], zs[half:])]
    turned = []
    for i, z in enumerate(lows):
        if i == 0:
            c = 1
        elif 4 * i == n:
            c = -1j
        else:
            c = np.exp(-2j * np.pi * i / n)
        turned.append(cmul_const(z, c))
    even, odd = small_fft(tops), small_fft(turned)
    out = [None] * n
    out[0::2], out[1::2] = even, odd
    return out


def tables(groups, local):
    length = groups * local
    s = np.arange(local, dtype=np.int64)
    base = 2 * np.pi * (np.outer(s, s) % local) / local
    turn = 2 * np.pi * np.outer(np.arange(groups, dtype=np.int64), s) / length
    scale = length ** -0.5
    f32 = lambda a: jnp.asarray(a.astype(np.float32))
    return (
        f32(np.cos(base) * scale),
        f32(np.sin(base) * scale),
        f32(np.cos(turn).reshape(groups, 1, local)),
        f32(np.sin(turn).reshape(groups, 1, local)),
    )


def exchange_kernel(
    n, local, chans, uniq,
    vis_ref, red_ref, cb_ref, sb_ref, tc_ref, ts_ref, out_ref,
    vis_buf, wt, avg, send1, recv1, spec, mh, ml, send2,
    load_sem, s1_sem, r1_sem, s2_sem, r2_sem, own1_sem, own2_sem,
):
    me = lax.axis_index("tm")
    halves = uniq // (n // chans) // LANES
    per_chan = n // chans
    tb = local // BLOCKS
    rows = tb * 2 * chans
    keep = local // n

    def load(i):
        return pltpu.make_async_copy(
            vis_ref.at[pl.ds(i * rows, rows), :], vis_buf.at[i], load_sem.at[i]
        )

    for i in range(BLOCKS):
        load(i).start()

    barrier = pltpu.get_barrier_semaphore()

    def greet(o, carry):
        pl.semaphore_signal(
            barrier, inc=1, device_id={"tm": lax.rem(me + o, n)}, device_id_type=MESH
        )
        return carry

    lax.fori_loop(1, n, greet, 0)

    wt[...] = (
        lax.broadcasted_iota(jnp.int32, wt.shape, 0) == red_ref[...]
    ).astype(jnp.float32).astype(jnp.bfloat16)
    ones = jnp.ones((8, wt.shape[1]), jnp.bfloat16)
    counts = lax.dot_general(ones, wt[...], NT, preferred_element_type=jnp.float32)
    inverse = 1.0 / counts[0:1]

    def slot(dest, h):
        return lax.rem(dest, per_chan) * halves + h, lax.div(dest, per_chan)

    def first(o, h, i):
        dest = lax.rem(me + o, n)
        lane_tile, chan = slot(dest, h)
        if h == 0:
            span = pl.ds(i * tb, tb)
            q = i
        else:
            span = pl.ds(0, local)
            q = BLOCKS + h - 1
        return pltpu.make_async_remote_copy(
            src_ref=send1.at[lane_tile, chan, :, span, :],
            dst_ref=recv1.at[h, me, :, span, :],
            send_sem=s1_sem.at[o, q],
            recv_sem=r1_sem.at[o, q],
            device_id={"tm": dest},
            device_id_type=MESH,
        )

    def own_first(h):
        lane_tile, chan = slot(me, h)
        return pltpu.make_async_copy(
            send1.at[lane_tile, chan], recv1.at[h, me], own1_sem.at[h]
        )

    def each(f):
        def body(o, carry):
            f(o)
            return carry
        lax.fori_loop(1, n, body, 0)

    for i in range(BLOCKS):
        load(i).wait()
        high, low = split_bf16(vis_buf[i])
        summed = lax.dot_general(high, wt[...], NT, preferred_element_type=jnp.float32)
        summed += lax.dot_general(low, wt[...], NT, preferred_element_type=jnp.float32)
        mean = summed * inverse
        for lt in range(uniq // LANES):
            avg[lt] = mean[:, lt * LANES:(lt + 1) * LANES]
        for lt in range(uniq // LANES):
            for f in range(chans):
                for p in range(2):
                    send1[lt, f, p, i * tb:(i + 1) * tb, :] = avg[
                        lt, pl.ds(p * chans + f, tb, stride=2 * chans), :
                    ]
        if i == 0:
            pl.semaphore_wait(barrier, n - 1)
        each(lambda o: first(o, 0, i).start())
    for h in range(1, halves):
        each(lambda o: first(o, h, 0).start())
    for h in range(halves):
        own_first(h).start()

    def make_matrix(e, carry):
        cosine = cb_ref[...] * tc_ref[e] - sb_ref[...] * ts_ref[e]
        sine = sb_ref[...] * tc_ref[e] + cb_ref[...] * ts_ref[e]
        ch, cl = split_bf16(cosine)
        sh, sl = split_bf16(sine)
        for target, c, s in ((mh, ch, sh), (ml, cl, sl)):
            target[e, 0:local, 0:local] = c
            target[e, 0:local, local:] = s
            target[e, local:, 0:local] = -s
            target[e, local:, local:] = c
        return carry

    lax.fori_loop(0, n, make_matrix, 0)

    def second(o, h):
        dest = lax.rem(me + o, n)
        return pltpu.make_async_remote_copy(
            src_ref=send2.at[h, dest],
            dst_ref=out_ref.at[h, me],
            send_sem=s2_sem.at[o, h],
            recv_sem=r2_sem.at[o, h],
            device_id={"tm": dest},
            device_id_type=MESH,
        )

    def own_second(h):
        return pltpu.make_async_copy(send2.at[h, me], out_ref.at[h, me], own2_sem.at[h])

    for h in range(halves):
        own_first(h).wait()
        if h == 0:
            for i in range(BLOCKS):
                each(lambda o: first(o, 0, i).wait_recv())
        else:
            each(lambda o: first(o, h, 0).wait_recv())

        def across(g, carry):
            at = pl.ds(pl.multiple_of(g * 8, 8), 8)
            zs = [(recv1[h, d, 0, at, :], recv1[h, d, 1, at, :]) for d in range(n)]
            for e, (re, im) in enumerate(small_fft(zs)):
                spec[e, 0, at, :] = re
                spec[e, 1, at, :] = im
            return carry

        lax.fori_loop(0, local // 8, across, 0)

        def within(e, carry):
            high, low = split_bf16(spec[e].reshape(2 * local, LANES))
            dot = functools.partial(jnp.dot, preferred_element_type=jnp.float32)
            value = dot(mh[e], high) + (dot(mh[e], low) + dot(ml[e], high))
            value = value.reshape(2, n, keep, LANES)
            for p in range(2):
                send2[h, :, e, p] = value[p]
            return carry

        lax.fori_loop(0, n, within, 0)
        each(lambda o: second(o, h).start())
        own_second(h).start()

    for i in range(BLOCKS):
        each(lambda o: first(o, 0, i).wait_send())
    for h in range(1, halves):
        each(lambda o: first(o, h, 0).wait_send())
    for h in range(halves):
        own_second(h).wait()
        each(lambda o: second(o, h).wait())


def project_kernel(
    n, local, chans, uniq, kept, got_ref, filt_ref, mm_ref, modes_ref, lay, part
):
    step = pl.program_id(0)
    per_chan = n // chans
    lane_tiles = uniq // LANES
    halves = lane_tiles // per_chan
    keep = local // n
    width = n * 2 * chans

    @pl.when(step == 0)
    def _():
        def place(e, carry):
            for h in range(halves):
                for j in range(n):
                    lt = (j % per_chan) * halves + h
                    for p in range(2):
                        start = (e * 2 + p) * chans + j // per_chan
                        lay[lt, pl.ds(start, keep, stride=width), :] = got_ref[h, j, e, p]
            return carry

        lax.fori_loop(0, n, place, 0)

    def one(m, carry):
        at = pl.multiple_of(step * width + m * 2 * chans, 2 * chans)
        real = jnp.zeros((kept, chans, LANES), jnp.float32)
        imag = jnp.zeros((kept, chans, LANES), jnp.float32)
        for lt in range(lane_tiles):
            cols = slice(lt * LANES, (lt + 1) * LANES)
            x0 = lay[lt, pl.ds(at, chans), :]
            x1 = lay[lt, pl.ds(at + chans, chans), :]
            mm_ref[m, 0, :, cols] = x0
            mm_ref[m, 1, :, cols] = x1
            x0 = x0.astype(jnp.bfloat16).astype(jnp.float32)[None]
            x1 = x1.astype(jnp.bfloat16).astype(jnp.float32)[None]
            f0 = filt_ref[m, 0, :, :, cols].astype(jnp.float32)
            f1 = filt_ref[m, 1, :, :, cols].astype(jnp.float32)
            real += f0 * x0 - f1 * x1
            imag += f0 * x1 + f1 * x0
        part[m, 0] = jnp.sum(real, axis=1)
        part[m, 1] = jnp.sum(imag, axis=1)
        return carry

    lax.fori_loop(0, n, one, 0)
    sums = part[...].reshape(n * 2 * kept, LANES)
    total = lax.dot_general(
        jnp.ones((8, LANES), jnp.float32), sums, NT,
        precision=lax.Precision.HIGHEST, preferred_element_type=jnp.float32,
    )
    modes_ref[0] = total[0:1]


def fits(n, local, chans, raw, uniq, kept):
    return (
        n % chans == 0
        and uniq % ((n // chans) * LANES) == 0
        and local % (8 * n) == 0
        and local % (8 * BLOCKS) == 0
        and local % LANES == 0
        and chans == 8
        and raw % LANES == 0
        and kept % 8 == 0
        and local == 8 * n
    )


def fused_device(visibilities, redundancy, mode_counts, filters):
    n = lax.axis_size("tm")
    local, _, chans, raw = visibilities.shape
    uniq, kept = filters.shape[4], filters.shape[2]
    halves = uniq // (n // chans) // LANES
    keep = local // n
    rows = local * 2 * chans
    vmem = pl.BlockSpec(memory_space=pltpu.VMEM)
    hbm = pl.BlockSpec(memory_space=pl.ANY)
    f32, bf16 = jnp.float32, jnp.bfloat16
    dma = pltpu.SemaphoreType.DMA
    got = pl.pallas_call(
        functools.partial(exchange_kernel, n, local, chans, uniq),
        out_shape=jax.ShapeDtypeStruct((halves, n, n, 2, keep, LANES), f32),
        in_specs=[hbm] + [vmem] * 5,
        out_specs=hbm,
        scratch_shapes=[
            pltpu.VMEM((BLOCKS, rows // BLOCKS, raw), f32),
            pltpu.VMEM((uniq, raw), bf16),
            pltpu.VMEM((uniq // LANES, rows // BLOCKS, LANES), f32),
            pltpu.VMEM((uniq // LANES, chans, 2, local, LANES), f32),
            pltpu.VMEM((halves, n, 2, local, LANES), f32),
            pltpu.VMEM((n, 2, local, LANES), f32),
            pltpu.VMEM((n, 2 * local, 2 * local), bf16),
            pltpu.VMEM((n, 2 * local, 2 * local), bf16),
            pltpu.VMEM((halves, n, n, 2, keep, LANES), f32),
            dma((BLOCKS,)),
            dma((n, BLOCKS + halves - 1)),
            dma((n, BLOCKS + halves - 1)),
            dma((n, halves)),
            dma((n, halves)),
            dma((halves,)),
            dma((halves,)),
        ],
        compiler_params=pltpu.CompilerParams(
            collective_id=0, has_side_effects=True, vmem_limit_bytes=60 * 2**20
        ),
        name="exchange",
    )(visibilities.reshape(rows, raw), redundancy.reshape(1, raw), *tables(n, local))
    width = n * 2 * chans
    mmodes, flat = pl.pallas_call(
        functools.partial(project_kernel, n, local, chans, uniq, kept),
        grid=(keep,),
        out_shape=(
            jax.ShapeDtypeStruct((local, 2, chans, uniq), f32),
            jax.ShapeDtypeStruct((keep, 1, n * 2 * kept), f32),
        ),
        in_specs=[
            pl.BlockSpec(got.shape, lambda k: (0,) * 6),
            pl.BlockSpec((n, 2, kept, chans, uniq), lambda k: (k, 0, 0, 0, 0)),
        ],
        out_specs=(
            pl.BlockSpec((n, 2, chans, uniq), lambda k: (k, 0, 0, 0)),
            pl.BlockSpec((1, 1, n * 2 * kept), lambda k: (k, 0, 0)),
        ),
        scratch_shapes=[
            pltpu.VMEM((uniq // LANES, keep * width, LANES), f32),
            pltpu.VMEM((n, 2, kept, LANES), f32),
        ],
        compiler_params=pltpu.CompilerParams(vmem_limit_bytes=56 * 2**20),
        name="project",
    )(got, filters)
    coefs = flat.reshape(local, 2, kept)
    kept_mask = lax.broadcasted_iota(jnp.int32, (local, kept), 1) < mode_counts[:, None]
    return mmodes, jnp.where(kept_mask[:, None, :], coefs, 0.0)


def phase_table(numer, period):
    phases = 2.0 * jnp.pi / period * numer.astype(jnp.float32)
    return (jnp.cos(phases), jnp.sin(phases))


def apply_stacked(cosine, sine_table, stacked, width):
    cos_part = jnp.dot(
        cosine, stacked, precision=lax.Precision.HIGHEST, preferred_element_type=jnp.float32
    )
    sin_part = jnp.dot(
        sine_table, stacked, precision=lax.Precision.HIGHEST, preferred_element_type=jnp.float32
    )
    real_out = cos_part[:, :width] + sin_part[:, width:]
    imag_out = cos_part[:, width:] - sin_part[:, :width]
    return jnp.concatenate([real_out, imag_out], axis=1)


def factored_transform(stacked, width):
    length = stacked.shape[0]
    radix_size = 64
    inner_size = length // radix_size
    outer_row = lax.broadcasted_iota(jnp.int32, (radix_size, radix_size), 0)
    outer_col = lax.broadcasted_iota(jnp.int32, (radix_size, radix_size), 1)
    cosine, sine_table = phase_table(outer_row * outer_col % radix_size, radix_size)
    grouped = stacked.reshape(radix_size, inner_size, 2, width)
    grouped = jnp.transpose(grouped, (0, 2, 1, 3)).reshape(radix_size, 2 * inner_size * width)
    section = apply_stacked(cosine, sine_table, grouped, inner_size * width)
    section = section.reshape(radix_size, 2, inner_size, width)
    section_real = section[:, 0]
    section_imag = section[:, 1]
    twist_row = lax.broadcasted_iota(jnp.int32, (radix_size, inner_size, 1), 0)
    twist_col = lax.broadcasted_iota(jnp.int32, (radix_size, inner_size, 1), 1)
    twist_cos, twist_sin = phase_table(twist_row * twist_col, length)
    turned_real = section_real * twist_cos + section_imag * twist_sin
    turned_imag = section_imag * twist_cos - section_real * twist_sin
    turned = jnp.stack([turned_real, turned_imag], axis=0)
    turned = jnp.transpose(turned, (2, 0, 1, 3)).reshape(inner_size, 2 * radix_size * width)
    inner_row = lax.broadcasted_iota(jnp.int32, (inner_size, inner_size), 0)
    inner_col = lax.broadcasted_iota(jnp.int32, (inner_size, inner_size), 1)
    cosine2, sine_table2 = phase_table(inner_row * inner_col % inner_size, inner_size)
    final = apply_stacked(cosine2, sine_table2, turned, radix_size * width)
    final = final.reshape(inner_size, 2, radix_size, width)
    return jnp.transpose(final, (0, 2, 1, 3)).reshape(length, 2 * width)


def transform(columns):
    length, _, width = columns.shape
    stacked = columns.reshape(length, 2 * width)
    result = factored_transform(stacked, width)
    scale = 1.0 / jnp.sqrt(jnp.float32(length))
    return (result * scale).reshape(length, 2, width)


def on_device(visibilities, redundancy, mode_counts, filters):
    groups = lax.axis_size("tm")
    local_times, _, channels, raw_count = visibilities.shape
    uniques = filters.shape[4]
    kept = filters.shape[2]
    if fits(groups, local_times, channels, raw_count, uniques, kept):
        return fused_device(visibilities, redundancy, mode_counts, filters)
    unique_block = uniques // groups
    members = (
        redundancy[:, None] == lax.broadcasted_iota(jnp.int32, (raw_count, uniques), 1)
    ).astype(jnp.float32)
    weights = members / jnp.sum(members, axis=0, keepdims=True)
    flat_rows = visibilities.reshape(local_times, 2 * channels, raw_count)
    blocked_weights = weights.reshape(raw_count, groups, unique_block)
    packed = jnp.einsum(
        "tqr,rjc->tjqc",
        flat_rows,
        blocked_weights,
        precision=lax.Precision.HIGHEST,
        preferred_element_type=jnp.float32,
    )
    packed = packed.reshape(local_times, groups, 2 * channels * unique_block)
    arrived = lax.all_to_all(packed, "tm", split_axis=1, concat_axis=0, tiled=True)
    length = arrived.shape[0]
    spectra = transform(arrived.reshape(length, 2, channels * unique_block))
    spectra = spectra.reshape(length, 1, 2 * channels * unique_block)
    regrouped = lax.all_to_all(spectra, "tm", split_axis=0, concat_axis=1, tiled=True)
    regrouped = regrouped.reshape(local_times, groups, 2, channels, unique_block)
    mmodes = jnp.transpose(regrouped, (0, 2, 3, 1, 4)).reshape(local_times, 2, channels, uniques)
    local_modes = mmodes.shape[0]
    rounded = mmodes.astype(jnp.bfloat16).reshape(local_modes, 2, channels * uniques)
    flat_filters = filters.reshape(local_modes, 2, kept, channels * uniques)
    products = jnp.einsum(
        "mpkc,mqc->mpqk", flat_filters, rounded, preferred_element_type=jnp.float32
    )
    real_out = products[:, 0, 0] - products[:, 1, 1]
    imag_out = products[:, 0, 1] + products[:, 1, 0]
    kept_mask = lax.broadcasted_iota(jnp.int32, (local_modes, kept), 1) < mode_counts[:, None]
    modes = jnp.where(kept_mask[:, None, :], jnp.stack([real_out, imag_out], axis=1), 0.0)
    return (mmodes, modes)


def solution(mesh):
    return jax.shard_map(
        on_device,
        mesh=mesh,
        in_specs=(P("tm", None, "grp", None), P("grp"), P("tm"), P("tm", None, None, "grp", None)),
        out_specs=(P("tm", None, "grp", None), P("tm", None, "grp")),
        check_vma=False,
    )
```

profile of v0, /device:TPU:13, one launch (start us, length us, event | category | flops | bytes accessed | tf_op | source)
XLA Modules:
  0.0 217.9 jit_solution(15463562015594316489)
XLA Ops:
  0.6 188.5 %exchange.1.got_ref = f32[2,16,16,2,8,128]{5,4,3,2,1,0:T(8,128)} custom-call(f32[2048,1024]{1,0:T(8,128)} %bitcast.2, s32[1,1024]{1,0:T(1,128)} %bitcast.3, f32[128,128]{1,0:T(8,128)} %constant.10.clone.cb_ref, f32[128,128]{1,0:T(8,128)} %constant.11.clone.sb_ref, f32[16,1,128]{2,1,0:T(1,128)} %constant.12.clone.tc_ref, f32[16,1,128]{2,1,0:T(1,128)} %constant.13.clone.ts_ref), custom_call_target="tpu_custom_call" | custom-call | tf_op jit(solution)/shard_map/exchange/pallas_call | solution.py:309
  189.2 0.0 copy-start
  189.2 26.9 %project.1 = (f32[128,2,8,512]{3,2,1,0:T(8,128)}, f32[8,1,512]{2,1,0:T(1,128)}) custom-call(f32[2,16,16,2,8,128]{5,4,3,2,1,0:T(8,128)} %exchange.1.got_ref, bf16[128,2,16,8,512]{4,3,2,1,0:T(8,128)(2,1)} %filt_ref.1), custom_call_target="tpu_custom_call" | custom-call | tf_op jit(solution)/shard_map/project/pallas_call | solution.py:338
  216.1 0.8 reduce
  216.8 0.2 reshape.30
  217.0 0.0 copy-done
  217.1 0.1 iota_compare_fusion
  217.2 0.1 broadcast_select_fusion
  217.3 0.7 copy.11
Async XLA Ops:
  189.2 27.9 %copy-start = (s32[128]{0:T(128)S(1)}, s32[128]{0:T(128)}, u32[]{:S(2)}) copy-start(s32[128]{0:T(128)} %param.10) | copy-start | bytes 1540
where the time goes:
time: 218 us
  Pallas kernels  215 us (99%)
    pallas_call x1, Pallas kernels, fused_device(): pl.pallas_call(functools.partial(exchange_kernel, n, local, chans, uniq),...  189 us
    pallas_call x1, Pallas kernels, fused_device(): pl.pallas_call(functools.partial(project_kernel, n, local, chans, uniq, k...  26.9 us

commit v1 on v0

--- a/solution.py
+++ b/solution.py
@@ -53,6 +53,15 @@
     return out
 
 
+def rounded(x):
+    return x.astype(jnp.bfloat16).astype(jnp.float32)[None]
+
+
+def late_tiles(n, chans, uniq):
+    halves = uniq // (n // chans) // LANES
+    return [t for t in range(uniq // LANES) if t % halves]
+
+
 def tables(groups, local):
     length = groups * local
     s = np.arange(local, dtype=np.int64)
@@ -69,10 +78,10 @@
 
 
 def exchange_kernel(
-    n, local, chans, uniq,
-    vis_ref, red_ref, cb_ref, sb_ref, tc_ref, ts_ref, out_ref,
-    vis_buf, wt, avg, send1, recv1, spec, mh, ml, send2,
-    load_sem, s1_sem, r1_sem, s2_sem, r2_sem, own1_sem, own2_sem,
+    n, local, chans, uniq, kept,
+    vis_ref, filt_ref, red_ref, cb_ref, sb_ref, tc_ref, ts_ref, out_ref, part_ref,
+    vis_buf, wt, avg, send1, recv1, spec, mh, ml, send2, filt, got, lay, part,
+    load_sem, s1_sem, r1_sem, s2_sem, r2_sem, own1_sem, own2_sem, filt_sem, got_sem, part_sem,
 ):
     me = lax.axis_index("tm")
     halves = uniq // (n // chans) // LANES
@@ -161,6 +170,17 @@
     for h in range(halves):
         own_first(h).start()
 
+    def fetch(k, c):
+        return pltpu.make_async_copy(
+            filt_ref.at[pl.ds(k * n, n), :, :, :, pl.ds(c * halves * LANES, LANES)],
+            filt.at[k, c],
+            filt_sem.at[k, c],
+        )
+
+    for k in range(keep):
+        for c in range(per_chan):
+            fetch(k, c).start()
+
     def make_matrix(e, carry):
         cosine = cb_ref[...] * tc_ref[e] - sb_ref[...] * ts_ref[e]
         sine = sb_ref[...] * tc_ref[e] + cb_ref[...] * ts_ref[e]
@@ -220,18 +240,65 @@
         each(lambda o: second(o, h).start())
         own_second(h).start()
 
+    own_second(0).wait()
+    each(lambda o: second(o, 0).wait_recv())
+    read = pltpu.make_async_copy(out_ref.at[0], got, got_sem)
+    read.start()
+    read.wait()
+    width = n * 2 * chans
+
+    def place(e, carry):
+        for j in range(n):
+            for p in range(2):
+                start = (e * 2 + p) * chans + j // per_chan
+                lay[j % per_chan, pl.ds(start, keep, stride=width), :] = got[j, e, p]
+        return carry
+
+    lax.fori_loop(0, n, place, 0)
+
+    def early(k, carry):
+        for c in range(per_chan):
+            fetch(k, c).wait()
+
+        def one(m, inner):
+            at = pl.multiple_of(k * width + m * 2 * chans, 2 * chans)
+            real = jnp.zeros((kept, chans, LANES), jnp.float32)
+            imag = jnp.zeros((kept, chans, LANES), jnp.float32)
+            for c in range(per_chan):
+                x0 = rounded(lay[c, pl.ds(at, chans), :])
+                x1 = rounded(lay[c, pl.ds(at + chans, chans), :])
+                f0 = filt[k, c, m, 0].astype(jnp.float32)
+                f1 = filt[k, c, m, 1].astype(jnp.float32)
+                real += f0 * x0 - f1 * x1
+                imag += f0 * x1 + f1 * x0
+            part[k * n + m, 0] = jnp.sum(real, axis=1)
+            part[k * n + m, 1] = jnp.sum(imag, axis=1)
+            return inner
+
+        lax.fori_loop(0, n, one, 0)
+        return carry
+
+    lax.fori_loop(0, keep, early, 0)
+    save = pltpu.make_async_copy(part, part_ref, part_sem)
+    save.start()
+
     for i in range(BLOCKS):
         each(lambda o: first(o, 0, i).wait_send())
     for h in range(1, halves):
         each(lambda o: first(o, h, 0).wait_send())
-    for h in range(halves):
+    each(lambda o: second(o, 0).wait_send())
+    for h in range(1, halves):
         own_second(h).wait()
         each(lambda o: second(o, h).wait())
+    save.wait()
 
 
 def project_kernel(
-    n, local, chans, uniq, kept, got_ref, filt_ref, mm_ref, modes_ref, lay, part
+    n, local, chans, uniq, kept, got_ref, early_ref, *refs
 ):
+    late = late_tiles(n, chans, uniq)
+    filt_refs = dict(zip(late, refs))
+    mm_ref, modes_ref, lay, part = refs[len(late):]
     step = pl.program_id(0)
     per_chan = n // chans
     lane_tiles = uniq // LANES
@@ -262,14 +329,15 @@
             x1 = lay[lt, pl.ds(at + chans, chans), :]
             mm_ref[m, 0, :, cols] = x0
             mm_ref[m, 1, :, cols] = x1
-            x0 = x0.astype(jnp.bfloat16).astype(jnp.float32)[None]
-            x1 = x1.astype(jnp.bfloat16).astype(jnp.float32)[None]
-            f0 = filt_ref[m, 0, :, :, cols].astype(jnp.float32)
-            f1 = filt_ref[m, 1, :, :, cols].astype(jnp.float32)
+            if lt not in filt_refs:
+                continue
+            x0, x1 = rounded(x0), rounded(x1)
+            f0 = filt_refs[lt][m, 0].astype(jnp.float32)
+            f1 = filt_refs[lt][m, 1].astype(jnp.float32)
             real += f0 * x0 - f1 * x1
             imag += f0 * x1 + f1 * x0
-        part[m, 0] = jnp.sum(real, axis=1)
-        part[m, 1] = jnp.sum(imag, axis=1)
+        part[m, 0] = jnp.sum(real, axis=1) + early_ref[m, 0]
+        part[m, 1] = jnp.sum(imag, axis=1) + early_ref[m, 1]
         return carry
 
     lax.fori_loop(0, n, one, 0)
@@ -306,11 +374,16 @@
     hbm = pl.BlockSpec(memory_space=pl.ANY)
     f32, bf16 = jnp.float32, jnp.bfloat16
     dma = pltpu.SemaphoreType.DMA
-    got = pl.pallas_call(
-        functools.partial(exchange_kernel, n, local, chans, uniq),
-        out_shape=jax.ShapeDtypeStruct((halves, n, n, 2, keep, LANES), f32),
-        in_specs=[hbm] + [vmem] * 5,
-        out_specs=hbm,
+    per_chan = n // chans
+    late = late_tiles(n, chans, uniq)
+    got, early = pl.pallas_call(
+        functools.partial(exchange_kernel, n, local, chans, uniq, kept),
+        out_shape=(
+            jax.ShapeDtypeStruct((halves, n, n, 2, keep, LANES), f32),
+            jax.ShapeDtypeStruct((local, 2, kept, LANES), f32),
+        ),
+        in_specs=[hbm] * 2 + [vmem] * 5,
+        out_specs=(hbm, hbm),
         scratch_shapes=[
             pltpu.VMEM((BLOCKS, rows // BLOCKS, raw), f32),
             pltpu.VMEM((uniq, raw), bf16),
@@ -321,6 +394,10 @@
             pltpu.VMEM((n, 2 * local, 2 * local), bf16),
             pltpu.VMEM((n, 2 * local, 2 * local), bf16),
             pltpu.VMEM((halves, n, n, 2, keep, LANES), f32),
+            pltpu.VMEM((keep, per_chan, n, 2, kept, chans, LANES), bf16),
+            pltpu.VMEM((n, n, 2, keep, LANES), f32),
+            pltpu.VMEM((per_chan, rows, LANES), f32),
+            pltpu.VMEM((local, 2, kept, LANES), f32),
             dma((BLOCKS,)),
             dma((n, BLOCKS + halves - 1)),
             dma((n, BLOCKS + halves - 1)),
@@ -328,12 +405,15 @@
             dma((n, halves)),
             dma((halves,)),
             dma((halves,)),
+            dma((keep, per_chan)),
+            dma,
+            dma,
         ],
         compiler_params=pltpu.CompilerParams(
             collective_id=0, has_side_effects=True, vmem_limit_bytes=60 * 2**20
         ),
         name="exchange",
-    )(visibilities.reshape(rows, raw), redundancy.reshape(1, raw), *tables(n, local))
+    )(visibilities.reshape(rows, raw), filters, redundancy.reshape(1, raw), *tables(n, local))
     width = n * 2 * chans
     mmodes, flat = pl.pallas_call(
         functools.partial(project_kernel, n, local, chans, uniq, kept),
@@ -344,7 +424,11 @@
         ),
         in_specs=[
             pl.BlockSpec(got.shape, lambda k: (0,) * 6),
-            pl.BlockSpec((n, 2, kept, chans, uniq), lambda k: (k, 0, 0, 0, 0)),
+            pl.BlockSpec((n, 2, kept, LANES), lambda k: (k, 0, 0, 0)),
+        ]
+        + [
+            pl.BlockSpec((n, 2, kept, chans, LANES), functools.partial(lambda t, k: (k, 0, 0, 0, t), t))
+            for t in late
         ],
         out_specs=(
             pl.BlockSpec((n, 2, chans, uniq), lambda k: (k, 0, 0, 0)),
@@ -356,7 +440,7 @@
         ],
         compiler_params=pltpu.CompilerParams(vmem_limit_bytes=56 * 2**20),
         name="project",
-    )(got, filters)
+    )(got, early, *[filters] * len(late))
     coefs = flat.reshape(local, 2, kept)
     kept_mask = lax.broadcasted_iota(jnp.int32, (local, kept), 1) < mode_counts[:, None]
     return mmodes, jnp.where(kept_mask[:, None, :], coefs, 0.0)

time: 218 us -> 212 us (0.972)
  Pallas kernels: 215 us -> 209 us
    pallas_call x1, Pallas kernels: 26.9 us -> 20.4 us  [fused_device(): pl.pallas_call(functools.partial(project_kernel, n, local, chans, uniq, k...]
where the time goes in v1:
time: 212 us
  Pallas kernels  209 us (99%)
    pallas_call x1, Pallas kernels, fused_device(): pl.pallas_call(functools.partial(exchange_kernel, n, local, chans, uniq,...  189 us
    pallas_call x1, Pallas kernels, fused_device(): pl.pallas_call(functools.partial(project_kernel, n, local, chans, uniq, k...  20.4 us

profile of v1, /device:TPU:13, one launch (start us, length us, event | category | flops | bytes accessed | tf_op | source)
XLA Modules:
  0.0 211.6 jit_solution(9821540934089472570)
XLA Ops:
  0.6 188.7 %exchange.1 = (f32[2,16,16,2,8,128]{5,4,3,2,1,0:T(8,128)}, f32[128,2,16,128]{3,2,1,0:T(8,128)}) custom-call(f32[2048,1024]{1,0:T(8,128)} %bitcast.2, bf16[128,2,16,8,512]{4,3,2,1,0:T(8,128)(2,1)} %refs_1_.1, s32[1,1024]{1,0:T(1,128)} %bitcast.3, f32[128,128]{1,0:T(8,128)} %constant.10.clone.cb_ref, f32[128,128]{1,0:T(8,128)} %constant.11.clone.sb_ref, ...), custom_call_target="tpu_custom_call" | custom-call | tf_op jit(solution)/shard_map/exchange/pallas_call | solution.py:379
  189.3 0.0 copy-start
  189.4 20.4 %project.1 = (f32[128,2,8,512]{3,2,1,0:T(8,128)}, f32[8,1,512]{2,1,0:T(1,128)}) custom-call(f32[2,16,16,2,8,128]{5,4,3,2,1,0:T(8,128)} %get-tuple-element.6.got_ref, f32[128,2,16,128]{3,2,1,0:T(8,128)} %get-tuple-element.7.early_ref, bf16[128,2,16,8,512]{4,3,2,1,0:T(8,128)(2,1)} %refs_1_.1, bf16[128,2,16,8,512]{4,3,2,1,0:T(8,128)(2,1)} %refs_1_.1), custom_call_target="tpu_custom_call" | custom-call | tf_op jit(solution)/shard_map/project/pallas_call | solution.py:418
  209.8 0.8 reduce
  210.5 0.2 reshape.30
  210.7 0.0 copy-done
  210.7 0.1 iota_compare_fusion
  210.8 0.1 broadcast_select_fusion
  210.9 0.7 copy.11
Async XLA Ops:
  189.3 21.4 %copy-start = (s32[128]{0:T(128)S(1)}, s32[128]{0:T(128)}, u32[]{:S(2)}) copy-start(s32[128]{0:T(128)} %param.10) | copy-start | bytes 1540
